TPU v7x, 32 devices: a whole 2x2x4 slice. The times are simulated.
32 devices in a mesh: row: 8 (over z, x), col: 4 (over y, core).
Axes of the slice: x: 2, y: 2, z: 4, core: 2. Of those that a mesh axis runs over, the one named last changes fastest.
Arguments:
- positions: float32 [3, 24576], P(None, ('row', 'col')), may hold values from -0.5 to 209.5, as said below
- widths: float32 [24576], P(('row', 'col')), may hold values from 0.8 to 1.6
- hardness: float32 [24576], P(('row', 'col')), may hold values from 16 to 48
- right_sides: float32 [64, 24576], P(None, ('row', 'col')), may hold values from -700 to 700
Outputs:
- charges: float32 [64, 24576], P(None, ('row', 'col'))
- residual: float32 [64, 24576], P(None, ('row', 'col'))
Inputs may be any that keep to these rules, and one draw needn't show every extreme that they name: `positions`: atoms sit near distinct sites of a lattice of spacing 2.2; any two atoms are 1.2 or more apart.
All inputs are finite; a program needn't handle non-finite values.
Results may differ from a plain program's by a relative error of at most 0.0003.
Values sent between devices are 32-bit elements; how exact they have to be, the bound alone decides.
No kernel may reach another device: no remote copies, remote signals or barrier semaphores. Data moves between devices by JAX's collectives and lax.ppermute only.
A program may use at most 128 MiB of HBM per device.

v0:
```python
import jax
import jax.numpy as jnp
from jax import lax
from jax.sharding import PartitionSpec as P

ITERS = 6
root_two = 1.4142135623730951
sqrt_pi = 1.7724538509055159


def kernel_block(pos_a, wid_a, pos_b, wid_b):
    squared = jnp.zeros((pos_a.shape[1], pos_b.shape[1]), jnp.float32)
    for axis_id in range(3):
        delta = pos_a[axis_id][:, None] - pos_b[axis_id][None, :]
        squared = squared + delta * delta
    distinct = squared > 0.25
    distance = jnp.sqrt(jnp.maximum(squared, 0.25))
    width_pair = jnp.sqrt(wid_a[:, None] * wid_a[:, None] + wid_b[None, :] * wid_b[None, :])
    coulomb = lax.erf(distance / (root_two * width_pair)) / distance
    return jnp.where(distinct, coulomb, 0.0)


def squared_norm(residual):
    return lax.psum(jnp.sum(residual * residual, axis=1), ("row", "col"))


def local(positions, widths, hardness, right_sides):
    diagonal = hardness + 1.0 / (widths * sqrt_pi)
    all_pos, all_wid = (
        lax.all_gather(positions, ("row", "col"), axis=1, tiled=True),
        lax.all_gather(widths, ("row", "col"), axis=0, tiled=True),
    )
    coupling = kernel_block(positions, widths, all_pos, all_wid)
    charges = jnp.zeros_like(right_sides)
    residual = right_sides
    search = right_sides
    norm_now = squared_norm(residual)
    for iteration in range(ITERS):
        summed = lax.dot_general(
            lax.all_gather(search, ("row", "col"), axis=1, tiled=True),
            coupling,
            (((1,), (1,)), ((), ())),
            precision=lax.Precision.HIGHEST,
            preferred_element_type=jnp.float32,
        )
        mapped = summed + diagonal[None, :] * search
        bending = lax.psum(jnp.sum(search * mapped, axis=1), ("row", "col"))
        step_len = norm_now / bending
        charges = charges + step_len[:, None] * search
        residual = residual - step_len[:, None] * mapped
        norm_next = squared_norm(residual)
        search = residual + (norm_next / norm_now)[:, None] * search
        norm_now = norm_next
    return (charges, residual)


def solution(mesh):
    in_specs = (
        P(None, ("row", "col")),
        P(("row", "col")),
        P(("row", "col")),
        P(None, ("row", "col")),
    )
    out_specs = (P(None, ("row", "col")), P(None, ("row", "col")))
    return jax.shard_map(local, mesh=mesh, in_specs=in_specs, out_specs=out_specs, check_vma=False)
```

profile of v0, /device:TPU:0, one launch (start us, length us, event | category | flops | bytes accessed | tf_op | source)
XLA Modules:
  0.0 1521.0 jit_solution(16570144204340177374)
XLA Ops:
  8.0 44.8 %all_gather.24 = f32[3,24576]{1,0:T(4,128)S(1)} all-gather(f32[3,768]{1,0:T(4,128)} %param.4), channel_id=1, replica_groups=mesh['row'=8,'col'=4] {'row','col'}, dimensions={1}, use_global_device_ids=true | all-gather | bytes 304128 | tf_op jit(solution)/shard_map/all_gather | solution.py:30
  55.3 37.7 %all-gather = f32[32,1,768]{2,1,0:T(1,128)S(1)} all-gather(f32[1,1,768]{2,1,0:T(1,128)S(1)} %reshape.23), channel_id=1, replica_groups=mesh['row'=8,'col'=4] {'row','col'}, dimensions={0}, use_global_device_ids=true | all-gather | bytes 101376 | tf_op jit(solution)/shard_map/all_gather | solution.py:31
  93.1 82.4 %fusion.19.clone.4 = f32[768,24576]{1,0:T(8,128)} fusion(f32[24576]{0:T(1024)S(1)} %bitcast.40, f32[768]{0:T(1024)S(1)} %get-tuple-element.21, f32[24576]{0:T(1024)S(1)} %bitcast.28, f32[768]{0:T(1024)S(1)} %get-tuple-element.5, f32[24576]{0:T(1024)S(1)} %bitcast.34, f32[768]{0:T(1024)S(1)} %get-tuple-element.6, ...), kind=kLoop, calls=%fused_computation.1.clone.5.clone.clone.clone.clone.clone.clone.clone.1 | loop fusion | flops 283115520 | bytes 75902976 | tf_op jit(solution)/shard_map/reduce_sum | solution.py:47
  175.5 78.1 %multiply_reduce_fusion.10 = (f32[64]{0:T(128)S(1)}, f32[64]{0:T(128)S(1)}, f32[64,768]{1,0:T(8,128)S(1)}) fusion(f32[64,768]{1,0:T(8,128)S(1)} %copy-done, f32[768]{0:T(1024)S(1)} %get-tuple-element.20, f32[64,24576]{1,0:T(8,128)} %all-gather.8.cloned.1.call-done, f32[768,24576]{1,0:T(8,128)} %fusion.19.clone.4), kind=kOutput, calls=%fused_computation.39 | convolution fusion | flops 14495809536 | bytes 82185728 | tf_op jit(solution)/shard_map/dot_general | solution.py:39
  291.0 42.4 %psum.86 = f32[64]{0:T(128)S(1)} all-reduce(f32[64]{0:T(128)S(1)} %multiply_reduce_fusion.9), channel_id=1, replica_groups=mesh['row'=8,'col'=4] {'row','col'}, use_global_device_ids=true, to_apply=%region_5.6 | all-reduce | flops 64 | bytes 512 | tf_op jit(solution)/shard_map/psum | solution.py:24
  334.2 82.4 %fusion.22.clone.2 = f32[768,24576]{1,0:T(8,128)} fusion(f32[24576]{0:T(1024)S(1)} %bitcast.41, f32[768]{0:T(1024)S(1)} %get-tuple-element.21, f32[24576]{0:T(1024)S(1)} %bitcast.29, f32[768]{0:T(1024)S(1)} %get-tuple-element.5, f32[24576]{0:T(1024)S(1)} %bitcast.35, f32[768]{0:T(1024)S(1)} %get-tuple-element.6, ...), kind=kLoop, calls=%fused_computation.1.clone.4.clone.clone.clone.clone.clone | loop fusion | flops 283115520 | bytes 75902976 | tf_op jit(solution)/shard_map/reduce_sum | solution.py:47
  416.6 78.3 %multiply_reduce_fusion.8 = (f32[64]{0:T(128)S(1)}, f32[64,768]{1,0:T(8,128)S(1)}) fusion(f32[64,768]{1,0:T(8,128)S(1)} %copy-done.2, f32[768]{0:T(1024)S(1)} %get-tuple-element.20, f32[64,24576]{1,0:T(8,128)} %all-gather.10.cloned.1.call-done, f32[768,24576]{1,0:T(8,128)} %fusion.22.clone.2), kind=kOutput, calls=%fused_computation.35 | convolution fusion | flops 14495711232 | bytes 82185472 | tf_op jit(solution)/shard_map/dot_general | solution.py:39
  494.9 38.3 %psum.87 = f32[64]{0:T(128)S(1)} all-reduce(f32[64]{0:T(128)S(1)} %get-tuple-element.25), channel_id=1, replica_groups=mesh['row'=8,'col'=4] {'row','col'}, use_global_device_ids=true, to_apply=%region_7.8 | all-reduce | flops 64 | bytes 512 | tf_op jit(solution)/shard_map/psum | solution.py:47
  533.5 41.6 %psum.88 = f32[64]{0:T(128)S(1)} all-reduce(f32[64]{0:T(128)S(1)} %get-tuple-element.15), channel_id=1, replica_groups=mesh['row'=8,'col'=4] {'row','col'}, use_global_device_ids=true, to_apply=%region_9.10 | all-reduce | flops 64 | bytes 512 | tf_op jit(solution)/shard_map/psum | solution.py:24
  575.9 93.9 %fusion.25.clone.2 = f32[768,24576]{1,0:T(8,128)} fusion(f32[24576]{0:T(1024)S(1)} %bitcast.42, f32[768]{0:T(1024)S(1)} %get-tuple-element.21, f32[24576]{0:T(1024)S(1)} %bitcast.30, f32[768]{0:T(1024)S(1)} %get-tuple-element.5, f32[24576]{0:T(1024)S(1)} %bitcast.36, f32[768]{0:T(1024)S(1)} %get-tuple-element.6, ...), kind=kLoop, calls=%fused_computation.1.clone.3.clone.clone.clone.clone.clone | loop fusion | flops 283115520 | bytes 75902976 | tf_op jit(solution)/shard_map/reduce_sum | solution.py:47
  669.8 78.3 %multiply_reduce_fusion.6 = (f32[64]{0:T(128)S(1)}, f32[64,768]{1,0:T(8,128)S(1)}) fusion(f32[64,768]{1,0:T(8,128)S(1)} %copy-done.4, f32[768]{0:T(1024)S(1)} %get-tuple-element.20, f32[64,24576]{1,0:T(8,128)} %all-gather.12.cloned.1.call-done, f32[768,24576]{1,0:T(8,128)} %fusion.25.clone.2), kind=kOutput, calls=%fused_computation.31 | convolution fusion | flops 14495711232 | bytes 82185472 | tf_op jit(solution)/shard_map/dot_general | solution.py:39
  748.1 38.4 %psum.89 = f32[64]{0:T(128)S(1)} all-reduce(f32[64]{0:T(128)S(1)} %get-tuple-element.27), channel_id=1, replica_groups=mesh['row'=8,'col'=4] {'row','col'}, use_global_device_ids=true, to_apply=%region_11.12 | all-reduce | flops 64 | bytes 512 | tf_op jit(solution)/shard_map/psum | solution.py:47
  786.7 41.5 %psum.90 = f32[64]{0:T(128)S(1)} all-reduce(f32[64]{0:T(128)S(1)} %get-tuple-element.13), channel_id=1, replica_groups=mesh['row'=8,'col'=4] {'row','col'}, use_global_device_ids=true, to_apply=%region_13.14 | all-reduce | flops 64 | bytes 512 | tf_op jit(solution)/shard_map/psum | solution.py:24
  829.1 82.8 %fusion.28.clone.2 = f32[768,24576]{1,0:T(8,128)} fusion(f32[24576]{0:T(1024)S(1)} %bitcast.43, f32[768]{0:T(1024)S(1)} %get-tuple-element.21, f32[24576]{0:T(1024)S(1)} %bitcast.31, f32[768]{0:T(1024)S(1)} %get-tuple-element.5, f32[24576]{0:T(1024)S(1)} %bitcast.37, f32[768]{0:T(1024)S(1)} %get-tuple-element.6, ...), kind=kLoop, calls=%fused_computation.1.clone.2.clone.clone.clone.clone.clone | loop fusion | flops 283115520 | bytes 75902976 | tf_op jit(solution)/shard_map/reduce_sum | solution.py:47
  911.9 78.3 %multiply_reduce_fusion.4 = (f32[64]{0:T(128)S(1)}, f32[64,768]{1,0:T(8,128)S(1)}) fusion(f32[64,768]{1,0:T(8,128)S(1)} %copy-done.6, f32[768]{0:T(1024)S(1)} %get-tuple-element.20, f32[64,24576]{1,0:T(8,128)} %all-gather.14.cloned.1.call-done, f32[768,24576]{1,0:T(8,128)} %fusion.28.clone.2), kind=kOutput, calls=%fused_computation.27 | convolution fusion | flops 14495711232 | bytes 82185472 | tf_op jit(solution)/shard_map/dot_general | solution.py:39
  990.2 38.5 %psum.91 = f32[64]{0:T(128)S(1)} all-reduce(f32[64]{0:T(128)S(1)} %get-tuple-element.29), channel_id=1, replica_groups=mesh['row'=8,'col'=4] {'row','col'}, use_global_device_ids=true, to_apply=%region_15.16 | all-reduce | flops 64 | bytes 512 | tf_op jit(solution)/shard_map/psum | solution.py:47
  1028.9 41.5 %psum.92 = f32[64]{0:T(128)S(1)} all-reduce(f32[64]{0:T(128)S(1)} %get-tuple-element.11), channel_id=1, replica_groups=mesh['row'=8,'col'=4] {'row','col'}, use_global_device_ids=true, to_apply=%region_17.18 | all-reduce | flops 64 | bytes 512 | tf_op jit(solution)/shard_map/psum | solution.py:24
  1071.2 82.6 %fusion.31.clone.2 = f32[768,24576]{1,0:T(8,128)} fusion(f32[24576]{0:T(1024)S(1)} %bitcast.44, f32[768]{0:T(1024)S(1)} %get-tuple-element.21, f32[24576]{0:T(1024)S(1)} %bitcast.32, f32[768]{0:T(1024)S(1)} %get-tuple-element.5, f32[24576]{0:T(1024)S(1)} %bitcast.38, f32[768]{0:T(1024)S(1)} %get-tuple-element.6, ...), kind=kLoop, calls=%fused_computation.1.clone.1.clone.clone.clone.clone.clone | loop fusion | flops 283115520 | bytes 75902976 | tf_op jit(solution)/shard_map/reduce_sum | solution.py:47
  1153.8 78.3 %multiply_reduce_fusion.2 = (f32[64]{0:T(128)S(1)}, f32[64,768]{1,0:T(8,128)S(1)}) fusion(f32[64,768]{1,0:T(8,128)S(1)} %copy-done.7, f32[768]{0:T(1024)S(1)} %get-tuple-element.20, f32[64,24576]{1,0:T(8,128)} %all-gather.16.cloned.1.call-done, f32[768,24576]{1,0:T(8,128)} %fusion.31.clone.2), kind=kOutput, calls=%fused_computation.23 | convolution fusion | flops 14495711232 | bytes 82185472 | tf_op jit(solution)/shard_map/dot_general | solution.py:39
  1232.1 38.6 %psum.93 = f32[64]{0:T(128)S(1)} all-reduce(f32[64]{0:T(128)S(1)} %get-tuple-element.31), channel_id=1, replica_groups=mesh['row'=8,'col'=4] {'row','col'}, use_global_device_ids=true, to_apply=%region_19.20 | all-reduce | flops 64 | bytes 512 | tf_op jit(solution)/shard_map/psum | solution.py:47
  1270.9 41.6 %psum.94 = f32[64]{0:T(128)S(1)} all-reduce(f32[64]{0:T(128)S(1)} %get-tuple-element.9), channel_id=1, replica_groups=mesh['row'=8,'col'=4] {'row','col'}, use_global_device_ids=true, to_apply=%region_21.22 | all-reduce | flops 64 | bytes 512 | tf_op jit(solution)/shard_map/psum | solution.py:24
  1313.3 82.4 %fusion.34.clone.4 = f32[768,24576]{1,0:T(8,128)} fusion(f32[24576]{0:T(1024)S(1)} %bitcast.45, f32[768]{0:T(1024)S(1)} %get-tuple-element.21, f32[24576]{0:T(1024)S(1)} %bitcast.33, f32[768]{0:T(1024)S(1)} %get-tuple-element.5, f32[24576]{0:T(1024)S(1)} %bitcast.39, f32[768]{0:T(1024)S(1)} %get-tuple-element.6, ...), kind=kLoop, calls=%fused_computation.1.clone.clone.clone.clone.clone.clone.1 | loop fusion | flops 283115520 | bytes 75902976 | tf_op jit(solution)/shard_map/reduce_sum | solution.py:47
  1395.8 78.4 %multiply_reduce_fusion = (f32[64]{0:T(128)S(1)}, f32[64,768]{1,0:T(8,128)S(1)}) fusion(f32[64,768]{1,0:T(8,128)S(1)} %copy-done.8, f32[768]{0:T(1024)S(1)} %get-tuple-element.20, f32[64,24576]{1,0:T(8,128)} %all-gather.18.cloned.1.call-done, f32[768,24576]{1,0:T(8,128)} %fusion.34.clone.4), kind=kOutput, calls=%fused_computation.19 | convolution fusion | flops 14495711232 | bytes 82185472 | tf_op jit(solution)/shard_map/dot_general | solution.py:39
  1474.2 38.7 %psum.95 = f32[64]{0:T(128)S(1)} all-reduce(f32[64]{0:T(128)S(1)} %get-tuple-element.33), channel_id=1, replica_groups=mesh['row'=8,'col'=4] {'row','col'}, use_global_device_ids=true, to_apply=%region_23.24 | all-reduce | flops 64 | bytes 512 | tf_op jit(solution)/shard_map/psum | solution.py:47
  (76 shorter events, 46.6 us)
Async XLA Ops:
  7.2 168.3 %copy-start = (f32[64,768]{1,0:T(8,128)S(1)}, f32[64,768]{1,0:T(8,128)}, u32[]{:S(2)}) copy-start(f32[64,768]{1,0:T(8,128)} %param.7) | copy-start | bytes 589828
  7.2 168.3 %all-gather.8.cloned.1.call-start = ((), (), s32[]{:S(2)}) async-start(), calls=%async_computation | async-start | bytes 6488064 | tf_op jit(solution)/shard_map/all_gather | solution.py:40
  7.9 408.7 %all-gather.10.cloned.1.call-start = ((), (), s32[]{:S(2)}) async-start(), calls=%async_computation.1 | async-start | bytes 6488064 | tf_op jit(solution)/shard_map/all_gather | solution.py:40
  290.8 242.5 %copy-start.9 = (f32[64]{0:T(128)}, f32[64]{0:T(128)S(1)}, u32[]{:S(2)}) copy-start(f32[64]{0:T(128)S(1)} %div.49) | copy-start | bytes 772
  334.1 82.5 %copy-start.2 = (f32[64,768]{1,0:T(8,128)S(1)}, f32[64,768]{1,0:T(8,128)}, u32[]{:S(2)}) copy-start(f32[64,768]{1,0:T(8,128)} %multiply_add_fusion.6) | copy-start | bytes 589828
  334.1 335.7 %all-gather.12.cloned.1.call-start = ((), (), s32[]{:S(2)}) async-start(), calls=%async_computation.2 | async-start | bytes 6488064 | tf_op jit(solution)/shard_map/all_gather | solution.py:40
  533.3 214.8 %copy-start.13 = (f32[64]{0:T(128)}, f32[64]{0:T(128)S(1)}, u32[]{:S(2)}) copy-start(f32[64]{0:T(128)S(1)} %div.51) | copy-start | bytes 772
  575.8 94.0 %copy-start.4 = (f32[64,768]{1,0:T(8,128)S(1)}, f32[64,768]{1,0:T(8,128)}, u32[]{:S(2)}) copy-start(f32[64,768]{1,0:T(8,128)} %multiply_add_fusion.5) | copy-start | bytes 589828
  575.9 336.1 %all-gather.14.cloned.1.call-start = ((), (), s32[]{:S(2)}) async-start(), calls=%async_computation.3 | async-start | bytes 6488064 | tf_op jit(solution)/shard_map/all_gather | solution.py:40
  786.5 203.7 %copy-start.11 = (f32[64]{0:T(128)}, f32[64]{0:T(128)S(1)}, u32[]{:S(2)}) copy-start(f32[64]{0:T(128)S(1)} %div.53) | copy-start | bytes 772
  829.0 82.9 %copy-start.6 = (f32[64,768]{1,0:T(8,128)S(1)}, f32[64,768]{1,0:T(8,128)}, u32[]{:S(2)}) copy-start(f32[64,768]{1,0:T(8,128)} %multiply_add_fusion.4) | copy-start | bytes 589828
  829.0 324.8 %all-gather.16.cloned.1.call-start = ((), (), s32[]{:S(2)}) async-start(), calls=%async_computation.4 | async-start | bytes 6488064 | tf_op jit(solution)/shard_map/all_gather | solution.py:40
  1071.2 82.7 %copy-start.7 = (f32[64,768]{1,0:T(8,128)S(1)}, f32[64,768]{1,0:T(8,128)}, u32[]{:S(2)}) copy-start(f32[64,768]{1,0:T(8,128)} %multiply_add_fusion.3) | copy-start | bytes 589828
  1071.2 324.6 %all-gather.18.cloned.1.call-start = ((), (), s32[]{:S(2)}) async-start(), calls=%async_computation.5 | async-start | bytes 6488064 | tf_op jit(solution)/shard_map/all_gather | solution.py:40
  1313.3 82.5 %copy-start.8 = (f32[64,768]{1,0:T(8,128)S(1)}, f32[64,768]{1,0:T(8,128)}, u32[]{:S(2)}) copy-start(f32[64,768]{1,0:T(8,128)} %multiply_add_fusion.2) | copy-start | bytes 589828
  1395.7 117.1 %copy-start.1 = (f32[64,768]{1,0:T(8,128)S(1)}, f32[64,768]{1,0:T(8,128)}, u32[]{:S(2)}) copy-start(f32[64,768]{1,0:T(8,128)} %param.7) | copy-start | bytes 589828
  1395.7 117.1 %copy-start.3 = (f32[64,768]{1,0:T(8,128)S(1)}, f32[64,768]{1,0:T(8,128)}, u32[]{:S(2)}) copy-start(f32[64,768]{1,0:T(8,128)} %multiply_add_fusion.6) | copy-start | bytes 589828
  1395.7 117.1 %copy-start.5 = (f32[64,768]{1,0:T(8,128)S(1)}, f32[64,768]{1,0:T(8,128)}, u32[]{:S(2)}) copy-start(f32[64,768]{1,0:T(8,128)} %multiply_add_fusion.5) | copy-start | bytes 589828
  1395.7 117.1 %copy-start.10 = (f32[64]{0:T(128)S(1)}, f32[64]{0:T(128)}, u32[]{:S(2)}) copy-start(f32[64]{0:T(128)} %copy-done.9) | copy-start | bytes 772
  1395.7 117.1 %copy-start.12 = (f32[64]{0:T(128)S(1)}, f32[64]{0:T(128)}, u32[]{:S(2)}) copy-start(f32[64]{0:T(128)} %copy-done.11) | copy-start | bytes 772
  1395.8 117.1 %copy-start.14 = (f32[64]{0:T(128)S(1)}, f32[64]{0:T(128)}, u32[]{:S(2)}) copy-start(f32[64]{0:T(128)} %copy-done.13) | copy-start | bytes 772
Sparse Core Ops, SparseCore 0:
  10.9 72.5 all-gather.7
  334.3 68.3 all-gather.9
  576.0 68.3 all-gather.11
  829.2 68.5 all-gather.13
  1071.3 68.5 all-gather.15
  1313.4 68.6 all-gather.17
where the time goes:
time: 1530 us; the launch traced here: 1520 us
  blocking collectives  521 us (34%)
  other arithmetic  513 us (34%)
  matrix products  470 us (31%)
    reduce_sum x6, other arithmetic, local(): bending = lax.psum(jnp.sum(search * mapped, axis=1), ('row', 'col'))  507 us
    dot_general x6, matrix products, local(): lax.dot_general(lax.all_gather(search, ('row', 'col'), axis=1, tiled=True...  470 us
    psum x6, blocking collectives, squared_norm(): return lax.psum(jnp.sum(residual * residual, axis=1), ('row', 'col'))  246 us
    psum x5, blocking collectives, local(): bending = lax.psum(jnp.sum(search * mapped, axis=1), ('row', 'col'))  192 us
    all_gather x1, blocking collectives, local(): lax.all_gather(positions, ('row', 'col'), axis=1, tiled=True)  44.8 us
    all_gather x1, blocking collectives, local(): lax.all_gather(widths, ('row', 'col'), axis=0, tiled=True)  37.7 us
  transfers between devices with their start and end apart: 6, of which 0 were waited for; matrix products, arithmetic and copies ran while one was open for 33% of the time, Pallas kernels for 0%

commit v1 on v0

--- a/solution.py
+++ b/solution.py
@@ -44,7 +44,7 @@
             preferred_element_type=jnp.float32,
         )
         mapped = summed + diagonal[None, :] * search
-        bending = lax.psum(jnp.sum(search * mapped, axis=1), ("row", "col"))
+        bending = lax.psum(lax.psum(jnp.sum(search * mapped, axis=1), "col"), "row")
         step_len = norm_now / bending
         charges = charges + step_len[:, None] * search
         residual = residual - step_len[:, None] * mapped

time: 1530 us -> 1480 us (0.967)
  blocking collectives: 521 us -> 465 us
    psum x5 -> x12, blocking collectives: 192 us -> 161 us  [local(): bending = lax.psum(lax.psum(jnp.sum(search * mapped, axis=1), 'col'), 'row')]
    psum x6, blocking collectives: 246 us -> 222 us  [squared_norm(): return lax.psum(jnp.sum(residual * residual, axis=1), ('row', 'col'))]
  transfers between devices with their start and end apart: 6 -> 6, of which waited for: 0 -> 0; matrix products, arithmetic and copies ran while one was open for 33% -> 35% of each run, Pallas kernels for 0% -> 0%
where the time goes in v1:
time: 1480 us; the launch traced here: 1460 us
  other arithmetic  513 us (35%)
  matrix products  470 us (32%)
  blocking collectives  465 us (31%)
    reduce_sum x6, other arithmetic, local(): bending = lax.psum(lax.psum(jnp.sum(search * mapped, axis=1), 'col'), 'row')  506 us
    dot_general x6, matrix products, local(): lax.dot_general(lax.all_gather(search, ('row', 'col'), axis=1, tiled=True...  470 us
    psum x6, blocking collectives, squared_norm(): return lax.psum(jnp.sum(residual * residual, axis=1), ('row', 'col'))  222 us
    psum x12, blocking collectives, local(): bending = lax.psum(lax.psum(jnp.sum(search * mapped, axis=1), 'col'), 'row')  161 us
    all_gather x1, blocking collectives, local(): lax.all_gather(positions, ('row', 'col'), axis=1, tiled=True)  44.8 us
    all_gather x1, blocking collectives, local(): lax.all_gather(widths, ('row', 'col'), axis=0, tiled=True)  37.7 us
  transfers between devices with their start and end apart: 6, of which 0 were waited for; matrix products, arithmetic and copies ran while one was open for 35% of the time, Pallas kernels for 0%

profile of v1, /device:TPU:0, one launch (start us, length us, event | category | flops | bytes accessed | tf_op | source)
XLA Modules:
  0.0 1464.9 jit_solution(10840282744595650860)
XLA Ops:
  8.0 44.8 %all_gather.24 = f32[3,24576]{1,0:T(4,128)S(1)} all-gather(f32[3,768]{1,0:T(4,128)} %param.4), channel_id=1, replica_groups=mesh['row'=8,'col'=4] {'row','col'}, dimensions={1}, use_global_device_ids=true | all-gather | bytes 304128 | tf_op jit(solution)/shard_map/all_gather | solution.py:30
  55.3 37.7 %all-gather = f32[32,1,768]{2,1,0:T(1,128)S(1)} all-gather(f32[1,1,768]{2,1,0:T(1,128)S(1)} %reshape.23), channel_id=1, replica_groups=mesh['row'=8,'col'=4] {'row','col'}, dimensions={0}, use_global_device_ids=true | all-gather | bytes 101376 | tf_op jit(solution)/shard_map/all_gather | solution.py:31
  93.1 82.4 %fusion.19.clone.4 = f32[768,24576]{1,0:T(8,128)} fusion(f32[24576]{0:T(1024)S(1)} %bitcast.40, f32[768]{0:T(1024)S(1)} %get-tuple-element.19, f32[24576]{0:T(1024)S(1)} %bitcast.28, f32[768]{0:T(1024)S(1)} %get-tuple-element.5, f32[24576]{0:T(1024)S(1)} %bitcast.34, f32[768]{0:T(1024)S(1)} %get-tuple-element.6, ...), kind=kLoop, calls=%fused_computation.1.clone.5.clone.clone.clone.clone.clone.clone.clone.1 | loop fusion | flops 283115520 | bytes 75902976 | tf_op jit(solution)/shard_map/reduce_sum | solution.py:47
  175.5 78.1 %multiply_reduce_fusion.10 = (f32[64]{0:T(128)S(1)}, f32[64]{0:T(128)S(1)}, f32[64,768]{1,0:T(8,128)S(1)}) fusion(f32[64,768]{1,0:T(8,128)S(1)} %copy-done, f32[768]{0:T(1024)S(1)} %get-tuple-element.18, f32[64,24576]{1,0:T(8,128)} %all-gather.8.cloned.1.call-done, f32[768,24576]{1,0:T(8,128)} %fusion.19.clone.4), kind=kOutput, calls=%fused_computation.39 | convolution fusion | flops 14495809536 | bytes 82185728 | tf_op jit(solution)/shard_map/dot_general | solution.py:39
  253.7 37.1 %psum.126 = f32[64]{0:T(128)S(1)} all-reduce(f32[64]{0:T(128)S(1)} %get-tuple-element.3), channel_id=1, replica_groups=mesh['row'=8,'col'=4] {'row','col'}, use_global_device_ids=true, to_apply=%region_1.2 | all-reduce | flops 64 | bytes 512 | tf_op jit(solution)/shard_map/psum | solution.py:24
  297.4 20.1 %psum.128 = f32[64]{0:T(128)S(1)} all-reduce(f32[64]{0:T(128)S(1)} %psum.127), channel_id=1, replica_groups=mesh['row'=8,'col'=4] {'row'}, use_global_device_ids=true, to_apply=%region_4.5 | all-reduce | flops 64 | bytes 512 | tf_op jit(solution)/shard_map/psum | solution.py:47
  317.7 36.9 %psum.129 = f32[64]{0:T(128)S(1)} all-reduce(f32[64]{0:T(128)S(1)} %multiply_reduce_fusion.9), channel_id=1, replica_groups=mesh['row'=8,'col'=4] {'row','col'}, use_global_device_ids=true, to_apply=%region_6.7 | all-reduce | flops 64 | bytes 512 | tf_op jit(solution)/shard_map/psum | solution.py:24
  355.4 82.4 %fusion.22.clone.2 = f32[768,24576]{1,0:T(8,128)} fusion(f32[24576]{0:T(1024)S(1)} %bitcast.41, f32[768]{0:T(1024)S(1)} %get-tuple-element.19, f32[24576]{0:T(1024)S(1)} %bitcast.29, f32[768]{0:T(1024)S(1)} %get-tuple-element.5, f32[24576]{0:T(1024)S(1)} %bitcast.35, f32[768]{0:T(1024)S(1)} %get-tuple-element.6, ...), kind=kLoop, calls=%fused_computation.1.clone.4.clone.clone.clone.clone.clone | loop fusion | flops 283115520 | bytes 75902976 | tf_op jit(solution)/shard_map/reduce_sum | solution.py:47
  437.9 78.3 %multiply_reduce_fusion.8 = (f32[64]{0:T(128)S(1)}, f32[64,768]{1,0:T(8,128)S(1)}) fusion(f32[64,768]{1,0:T(8,128)S(1)} %copy-done.2, f32[768]{0:T(1024)S(1)} %get-tuple-element.18, f32[64,24576]{1,0:T(8,128)} %all-gather.10.cloned.1.call-done, f32[768,24576]{1,0:T(8,128)} %fusion.22.clone.2), kind=kOutput, calls=%fused_computation.35 | convolution fusion | flops 14495711232 | bytes 82185472 | tf_op jit(solution)/shard_map/dot_general | solution.py:39
  523.0 19.9 %psum.131 = f32[64]{0:T(128)S(1)} all-reduce(f32[64]{0:T(128)S(1)} %psum.130), channel_id=1, replica_groups=mesh['row'=8,'col'=4] {'row'}, use_global_device_ids=true, to_apply=%region_9.10 | all-reduce | flops 64 | bytes 512 | tf_op jit(solution)/shard_map/psum | solution.py:47
  543.1 36.8 %psum.132 = f32[64]{0:T(128)S(1)} all-reduce(f32[64]{0:T(128)S(1)} %get-tuple-element.13), channel_id=1, replica_groups=mesh['row'=8,'col'=4] {'row','col'}, use_global_device_ids=true, to_apply=%region_11.12 | all-reduce | flops 64 | bytes 512 | tf_op jit(solution)/shard_map/psum | solution.py:24
  580.8 93.6 %fusion.25.clone.2 = f32[768,24576]{1,0:T(8,128)} fusion(f32[24576]{0:T(1024)S(1)} %bitcast.42, f32[768]{0:T(1024)S(1)} %get-tuple-element.19, f32[24576]{0:T(1024)S(1)} %bitcast.30, f32[768]{0:T(1024)S(1)} %get-tuple-element.5, f32[24576]{0:T(1024)S(1)} %bitcast.36, f32[768]{0:T(1024)S(1)} %get-tuple-element.6, ...), kind=kLoop, calls=%fused_computation.1.clone.3.clone.clone.clone.clone.clone | loop fusion | flops 283115520 | bytes 75902976 | tf_op jit(solution)/shard_map/reduce_sum | solution.py:47
  674.4 78.3 %multiply_reduce_fusion.6 = (f32[64]{0:T(128)S(1)}, f32[64,768]{1,0:T(8,128)S(1)}) fusion(f32[64,768]{1,0:T(8,128)S(1)} %copy-done.4, f32[768]{0:T(1024)S(1)} %get-tuple-element.18, f32[64,24576]{1,0:T(8,128)} %all-gather.12.cloned.1.call-done, f32[768,24576]{1,0:T(8,128)} %fusion.25.clone.2), kind=kOutput, calls=%fused_computation.31 | convolution fusion | flops 14495711232 | bytes 82185472 | tf_op jit(solution)/shard_map/dot_general | solution.py:39
  759.6 19.8 %psum.134 = f32[64]{0:T(128)S(1)} all-reduce(f32[64]{0:T(128)S(1)} %psum.133), channel_id=1, replica_groups=mesh['row'=8,'col'=4] {'row'}, use_global_device_ids=true, to_apply=%region_14.15 | all-reduce | flops 64 | bytes 512 | tf_op jit(solution)/shard_map/psum | solution.py:47
  779.7 36.9 %psum.135 = f32[64]{0:T(128)S(1)} all-reduce(f32[64]{0:T(128)S(1)} %get-tuple-element.11), channel_id=1, replica_groups=mesh['row'=8,'col'=4] {'row','col'}, use_global_device_ids=true, to_apply=%region_16.17 | all-reduce | flops 64 | bytes 512 | tf_op jit(solution)/shard_map/psum | solution.py:24
  817.4 82.8 %fusion.28.clone.2 = f32[768,24576]{1,0:T(8,128)} fusion(f32[24576]{0:T(1024)S(1)} %bitcast.43, f32[768]{0:T(1024)S(1)} %get-tuple-element.19, f32[24576]{0:T(1024)S(1)} %bitcast.31, f32[768]{0:T(1024)S(1)} %get-tuple-element.5, f32[24576]{0:T(1024)S(1)} %bitcast.37, f32[768]{0:T(1024)S(1)} %get-tuple-element.6, ...), kind=kLoop, calls=%fused_computation.1.clone.2.clone.clone.clone.clone.clone | loop fusion | flops 283115520 | bytes 75902976 | tf_op jit(solution)/shard_map/reduce_sum | solution.py:47
  900.2 78.3 %multiply_reduce_fusion.4 = (f32[64]{0:T(128)S(1)}, f32[64,768]{1,0:T(8,128)S(1)}) fusion(f32[64,768]{1,0:T(8,128)S(1)} %copy-done.6, f32[768]{0:T(1024)S(1)} %get-tuple-element.18, f32[64,24576]{1,0:T(8,128)} %all-gather.14.cloned.1.call-done, f32[768,24576]{1,0:T(8,128)} %fusion.28.clone.2), kind=kOutput, calls=%fused_computation.27 | convolution fusion | flops 14495711232 | bytes 82185472 | tf_op jit(solution)/shard_map/dot_general | solution.py:39
  985.5 19.8 %psum.137 = f32[64]{0:T(128)S(1)} all-reduce(f32[64]{0:T(128)S(1)} %psum.136), channel_id=1, replica_groups=mesh['row'=8,'col'=4] {'row'}, use_global_device_ids=true, to_apply=%region_19.20 | all-reduce | flops 64 | bytes 512 | tf_op jit(solution)/shard_map/psum | solution.py:47
  1005.5 36.9 %psum.138 = f32[64]{0:T(128)S(1)} all-reduce(f32[64]{0:T(128)S(1)} %get-tuple-element.9), channel_id=1, replica_groups=mesh['row'=8,'col'=4] {'row','col'}, use_global_device_ids=true, to_apply=%region_21.22 | all-reduce | flops 64 | bytes 512 | tf_op jit(solution)/shard_map/psum | solution.py:24
  1043.3 82.6 %fusion.31.clone.2 = f32[768,24576]{1,0:T(8,128)} fusion(f32[24576]{0:T(1024)S(1)} %bitcast.44, f32[768]{0:T(1024)S(1)} %get-tuple-element.19, f32[24576]{0:T(1024)S(1)} %bitcast.32, f32[768]{0:T(1024)S(1)} %get-tuple-element.5, f32[24576]{0:T(1024)S(1)} %bitcast.38, f32[768]{0:T(1024)S(1)} %get-tuple-element.6, ...), kind=kLoop, calls=%fused_computation.1.clone.1.clone.clone.clone.clone.clone | loop fusion | flops 283115520 | bytes 75902976 | tf_op jit(solution)/shard_map/reduce_sum | solution.py:47
  1125.9 78.3 %multiply_reduce_fusion.2 = (f32[64]{0:T(128)S(1)}, f32[64,768]{1,0:T(8,128)S(1)}) fusion(f32[64,768]{1,0:T(8,128)S(1)} %copy-done.7, f32[768]{0:T(1024)S(1)} %get-tuple-element.18, f32[64,24576]{1,0:T(8,128)} %all-gather.16.cloned.1.call-done, f32[768,24576]{1,0:T(8,128)} %fusion.31.clone.2), kind=kOutput, calls=%fused_computation.23 | convolution fusion | flops 14495711232 | bytes 82185472 | tf_op jit(solution)/shard_map/dot_general | solution.py:39
  1231.1 37.1 %psum.141 = f32[64]{0:T(128)S(1)} all-reduce(f32[64]{0:T(128)S(1)} %get-tuple-element.7), channel_id=1, replica_groups=mesh['row'=8,'col'=4] {'row','col'}, use_global_device_ids=true, to_apply=%region_26.27 | all-reduce | flops 64 | bytes 512 | tf_op jit(solution)/shard_map/psum | solution.py:24
  1269.0 82.4 %fusion.34.clone.4 = f32[768,24576]{1,0:T(8,128)} fusion(f32[24576]{0:T(1024)S(1)} %bitcast.45, f32[768]{0:T(1024)S(1)} %get-tuple-element.19, f32[24576]{0:T(1024)S(1)} %bitcast.33, f32[768]{0:T(1024)S(1)} %get-tuple-element.5, f32[24576]{0:T(1024)S(1)} %bitcast.39, f32[768]{0:T(1024)S(1)} %get-tuple-element.6, ...), kind=kLoop, calls=%fused_computation.1.clone.clone.clone.clone.clone.clone.1 | loop fusion | flops 283115520 | bytes 75902976 | tf_op jit(solution)/shard_map/reduce_sum | solution.py:47
  1351.6 78.4 %multiply_reduce_fusion = (f32[64]{0:T(128)S(1)}, f32[64,768]{1,0:T(8,128)S(1)}) fusion(f32[64,768]{1,0:T(8,128)S(1)} %copy-done.8, f32[768]{0:T(1024)S(1)} %get-tuple-element.18, f32[64,24576]{1,0:T(8,128)} %all-gather.18.cloned.1.call-done, f32[768,24576]{1,0:T(8,128)} %fusion.34.clone.4), kind=kOutput, calls=%fused_computation.19 | convolution fusion | flops 14495711232 | bytes 82185472 | tf_op jit(solution)/shard_map/dot_general | solution.py:39
  (83 shorter events, 90.4 us)
Async XLA Ops:
  7.2 168.3 %copy-start = (f32[64,768]{1,0:T(8,128)S(1)}, f32[64,768]{1,0:T(8,128)}, u32[]{:S(2)}) copy-start(f32[64,768]{1,0:T(8,128)} %param.7) | copy-start | bytes 589828
  7.2 168.3 %all-gather.8.cloned.1.call-start = ((), (), s32[]{:S(2)}) async-start(), calls=%async_computation | async-start | bytes 6488064 | tf_op jit(solution)/shard_map/all_gather | solution.py:40
  7.9 430.0 %all-gather.10.cloned.1.call-start = ((), (), s32[]{:S(2)}) async-start(), calls=%async_computation.1 | async-start | bytes 6488064 | tf_op jit(solution)/shard_map/all_gather | solution.py:40
  317.5 225.4 %copy-start.9 = (f32[64]{0:T(128)}, f32[64]{0:T(128)S(1)}, u32[]{:S(2)}) copy-start(f32[64]{0:T(128)S(1)} %div.49) | copy-start | bytes 772
  355.4 82.5 %copy-start.2 = (f32[64,768]{1,0:T(8,128)S(1)}, f32[64,768]{1,0:T(8,128)}, u32[]{:S(2)}) copy-start(f32[64,768]{1,0:T(8,128)} %multiply_add_fusion.6) | copy-start | bytes 589828
  355.4 319.0 %all-gather.12.cloned.1.call-start = ((), (), s32[]{:S(2)}) async-start(), calls=%async_computation.2 | async-start | bytes 6488064 | tf_op jit(solution)/shard_map/all_gather | solution.py:40
  542.9 209.7 %copy-start.13 = (f32[64]{0:T(128)}, f32[64]{0:T(128)S(1)}, u32[]{:S(2)}) copy-start(f32[64]{0:T(128)S(1)} %div.51) | copy-start | bytes 772
  580.7 93.6 %copy-start.4 = (f32[64,768]{1,0:T(8,128)S(1)}, f32[64,768]{1,0:T(8,128)}, u32[]{:S(2)}) copy-start(f32[64,768]{1,0:T(8,128)} %multiply_add_fusion.5) | copy-start | bytes 589828
  580.8 319.4 %all-gather.14.cloned.1.call-start = ((), (), s32[]{:S(2)}) async-start(), calls=%async_computation.3 | async-start | bytes 6488064 | tf_op jit(solution)/shard_map/all_gather | solution.py:40
  779.5 199.1 %copy-start.11 = (f32[64]{0:T(128)}, f32[64]{0:T(128)S(1)}, u32[]{:S(2)}) copy-start(f32[64]{0:T(128)S(1)} %div.53) | copy-start | bytes 772
  817.3 82.9 %copy-start.6 = (f32[64,768]{1,0:T(8,128)S(1)}, f32[64,768]{1,0:T(8,128)}, u32[]{:S(2)}) copy-start(f32[64,768]{1,0:T(8,128)} %multiply_add_fusion.4) | copy-start | bytes 589828
  817.3 308.5 %all-gather.16.cloned.1.call-start = ((), (), s32[]{:S(2)}) async-start(), calls=%async_computation.4 | async-start | bytes 6488064 | tf_op jit(solution)/shard_map/all_gather | solution.py:40
  1043.2 82.7 %copy-start.7 = (f32[64,768]{1,0:T(8,128)S(1)}, f32[64,768]{1,0:T(8,128)}, u32[]{:S(2)}) copy-start(f32[64,768]{1,0:T(8,128)} %multiply_add_fusion.3) | copy-start | bytes 589828
  1043.2 308.3 %all-gather.18.cloned.1.call-start = ((), (), s32[]{:S(2)}) async-start(), calls=%async_computation.5 | async-start | bytes 6488064 | tf_op jit(solution)/shard_map/all_gather | solution.py:40
  1269.0 82.5 %copy-start.8 = (f32[64,768]{1,0:T(8,128)S(1)}, f32[64,768]{1,0:T(8,128)}, u32[]{:S(2)}) copy-start(f32[64,768]{1,0:T(8,128)} %multiply_add_fusion.2) | copy-start | bytes 589828
  1351.5 105.3 %copy-start.1 = (f32[64,768]{1,0:T(8,128)S(1)}, f32[64,768]{1,0:T(8,128)}, u32[]{:S(2)}) copy-start(f32[64,768]{1,0:T(8,128)} %param.7) | copy-start | bytes 589828
  1351.5 105.3 %copy-start.3 = (f32[64,768]{1,0:T(8,128)S(1)}, f32[64,768]{1,0:T(8,128)}, u32[]{:S(2)}) copy-start(f32[64,768]{1,0:T(8,128)} %multiply_add_fusion.6) | copy-start | bytes 589828
  1351.5 105.3 %copy-start.5 = (f32[64,768]{1,0:T(8,128)S(1)}, f32[64,768]{1,0:T(8,128)}, u32[]{:S(2)}) copy-start(f32[64,768]{1,0:T(8,128)} %multiply_add_fusion.5) | copy-start | bytes 589828
  1351.5 105.3 %copy-start.10 = (f32[64]{0:T(128)S(1)}, f32[64]{0:T(128)}, u32[]{:S(2)}) copy-start(f32[64]{0:T(128)} %copy-done.9) | copy-start | bytes 772
  1351.5 105.3 %copy-start.12 = (f32[64]{0:T(128)S(1)}, f32[64]{0:T(128)}, u32[]{:S(2)}) copy-start(f32[64]{0:T(128)} %copy-done.11) | copy-start | bytes 772
  1351.5 105.3 %copy-start.14 = (f32[64]{0:T(128)S(1)}, f32[64]{0:T(128)}, u32[]{:S(2)}) copy-start(f32[64]{0:T(128)} %copy-done.13) | copy-start | bytes 772
Sparse Core Ops, SparseCore 0:
  10.9 72.5 all-gather.7
  355.5 70.8 all-gather.9
  580.9 71.0 all-gather.11
  817.5 71.0 all-gather.13
  1043.3 71.1 all-gather.15
  1269.2 71.1 all-gather.17
